TPU v7x, 32 devices: a whole 2x2x4 slice. The times are simulated.
32 devices in a mesh: grp: 2 (over y), seq: 16 (over z, x, core).
Axes of the slice: x: 2, y: 2, z: 4, core: 2. Of those that a mesh axis runs over, the one named last changes fastest.
Arguments:
- hidden: bfloat16 [16, 4096], P('grp'), parts along dimension 0, may hold values from -6 to 6
- mix_gain: float32 [4096], replicated, may hold values from 0.5 to 1.5
- in_gate_input: bfloat16 [4096, 2048], P(None, 'seq'), may hold values from -0.09375 to 0.09375
- in_step: bfloat16 [4096, 16], P(None, 'seq'), may hold values from -0.09375 to 0.09375
- in_groups: bfloat16 [4096, 2048], P(None, 'seq'), may hold values from -0.09375 to 0.09375
- conv_input: bfloat16 [16, 3, 1024], P('grp', None, 'seq'), parts along dimension 0, may hold values from -6 to 6
- conv_groups: bfloat16 [16, 3, 2048], P('grp', None, 'seq'), parts along dimension 0, may hold values from -6 to 6
- taps_input: float32 [5, 1024], P(None, 'seq'), may hold values from -0.6 to 0.6
- taps_groups: float32 [5, 2048], P(None, 'seq'), may hold values from -0.6 to 0.6
- decay_rate: float32 [16], P('seq'), may hold values from 1 to 16
- step_bias: float32 [16], P('seq'), may hold values from -4 to -1
- skip_gain: float32 [16], P('seq'), may hold values from 0.1 to 1.9
- norm_gain: float32 [1024], P('seq'), may hold values from 0.5 to 1.5
- out_mixer: bfloat16 [1024, 4096], P('seq'), may hold values from -0.1875 to 0.1875
- ssm_state: float32 [16, 16, 64, 128], P('grp', 'seq'), parts along dimension 0, may hold values from -6 to 6
- attn_gain: float32 [4096], P('seq'), may hold values from 0.5 to 1.5
- w_qkv: bfloat16 [4096, 6144], P('seq'), may hold values from -0.09375 to 0.09375
- w_out: bfloat16 [4096, 4096], P(None, 'seq'), may hold values from -0.09375 to 0.09375
- kv_cache: bfloat16 [64, 128, 2048], P(('grp', 'seq')), parts along dimension 0, may hold values from -310 to 310
- page_table: int32 [16, 4], P('grp'), parts along dimension 0, may hold values from 0 to 31, as said below
- lengths: int32 [16], P('grp'), parts along dimension 0, may hold values from 1 to 512
Outputs:
- final: bfloat16 [16, 4096], P('grp', 'seq'), parts along dimension 0
- new_state: float32 [16, 16, 64, 128], P('grp', 'seq'), parts along dimension 0
- new_kv: bfloat16 [16, 2048], P('grp'), parts along dimension 0
There are 2 independent parts, one for each index of `grp`. A program takes and returns all parts, laid end to end along the dimension named above; an argument that names none is the same for every part. Nothing has to cross between parts.
Inputs may be any that keep to these rules, and one draw needn't show every extreme that they name: `page_table`: each number 0 to 31 appears exactly once.
All inputs are finite; a program needn't handle non-finite values.
Results may differ from a plain program's by a relative error of at most 0.018.
Values may be sent and summed in bfloat16 or wider, within the bound.
No kernel may reach another device: no remote copies, remote signals or barrier semaphores. Data moves between devices by JAX's collectives and lax.ppermute only.
A program may use at most 64 MiB of HBM per device.

v0:
```python
import jax
import jax.numpy as jnp
from jax import lax
from jax.sharding import PartitionSpec as P

QH = 32
KVH = 8
HD = 128
STATE = 128
GROUPS = 8
epsilon = 1e-05
lowest = -1e30


def merged(array, axis, combine):
    everything = jax.tree.map(
        lambda part, kind: lax.all_gather(part.astype(kind), axis),
        array,
        (jnp.bfloat16, jnp.bfloat16, jnp.bfloat16),
    )

    def take(k):
        return jax.tree.map(lambda part, own: part[k].astype(own.dtype), everything, array)

    return lax.fori_loop(
        1, lax.axis_size(axis), lambda k, so_far: combine(so_far, take(k)), take(0)
    )


def conv_step(state, fresh, taps):
    window = jnp.concatenate([state.astype(jnp.float32), fresh[:, None, :]], axis=1)
    summed = jnp.sum(window * taps[:-1][None], axis=1) + taps[-1][None]
    return jax.nn.silu(summed)


def merge_pair(first, second):
    peak = jnp.maximum(first[0], second[0])
    first_factor = jnp.exp(first[0] - peak)
    second_factor = jnp.exp(second[0] - peak)
    total = first[1] * first_factor + second[1] * second_factor
    values = first[2] * first_factor[..., None] + second[2] * second_factor[..., None]
    return (peak, total, values)


def finish(peak_prior, total_prior, values_prior, query_rows, key_rows, value_rows, scale):
    own = jnp.sum(query_rows.astype(jnp.float32) * key_rows.astype(jnp.float32), axis=-1) * scale
    peak = jnp.maximum(peak_prior, own)
    old_factor = jnp.exp(peak_prior - peak)
    own_weight = jnp.exp(own - peak)
    summed = values_prior * old_factor[..., None] + own_weight[..., None] * value_rows.astype(
        jnp.float32
    )
    return (summed / (total_prior * old_factor + own_weight)[..., None]).astype(jnp.bfloat16)


def shards(
    hidden,
    mix_gain,
    in_gate_input,
    in_step,
    in_groups,
    conv_input,
    conv_groups,
    taps_input,
    taps_groups,
    decay_rate,
    step_bias,
    skip_gain,
    norm_gain,
    out_mixer,
    ssm_state,
    attn_gain,
    w_qkv,
    w_out,
    kv_cache,
    page_table,
    lengths,
):
    highest = lax.Precision.HIGHEST
    count_seq = lax.axis_size("seq")
    position = lax.axis_index("seq")
    requests = hidden.shape[0]
    width = hidden.shape[1]
    heads_here = in_step.shape[1]
    head_width = in_gate_input.shape[1] // (2 * heads_here)
    heads_total = heads_here * count_seq
    per_group = heads_total // GROUPS
    stream = hidden.astype(jnp.float32)
    normed = (
        stream * lax.rsqrt(jnp.mean(stream * stream, axis=-1, keepdims=True) + epsilon) * mix_gain
    ).astype(jnp.bfloat16)
    gate_input = jnp.dot(normed, in_gate_input, preferred_element_type=jnp.float32).reshape(
        requests, heads_here, 2, head_width
    )
    gate_part = gate_input[:, :, 0]
    input_part = gate_input[:, :, 1].reshape(requests, heads_here * head_width)
    step_raw = jnp.dot(normed, in_step, preferred_element_type=jnp.float32)
    group_raw = jnp.dot(normed, in_groups, preferred_element_type=jnp.float32)
    conv_out = conv_step(conv_input, input_part, taps_input).reshape(
        requests, heads_here, head_width
    )
    group_conv = conv_step(conv_groups, group_raw, taps_groups).astype(jnp.bfloat16)
    group_all = lax.all_gather(group_conv, "seq", axis=1, tiled=True).astype(jnp.float32)
    inject = group_all[:, : GROUPS * STATE].reshape(requests, GROUPS, STATE)
    readout = group_all[:, GROUPS * STATE :].reshape(requests, GROUPS, STATE)
    head_ids = position * heads_here + jnp.arange(heads_here, dtype=jnp.int32)
    select = (head_ids[:, None] % GROUPS == jnp.arange(GROUPS, dtype=jnp.int32)[None, :]).astype(
        jnp.float32
    )
    inject_heads = jnp.einsum("hg,rgn->rhn", select, inject, precision=highest)
    readout_heads = jnp.einsum("hg,rgn->rhn", select, readout, precision=highest)
    step_size = jax.nn.softplus(step_raw + step_bias)
    decay = jnp.exp(-decay_rate * step_size)
    new_state = (
        decay[:, :, None, None] * ssm_state
        + (step_size[:, :, None] * conv_out)[:, :, :, None] * inject_heads[:, :, None, :]
    )
    ssm_out = (
        jnp.einsum("rhpn,rhn->rhp", new_state, readout_heads, precision=highest)
        + skip_gain[None, :, None] * conv_out
    )
    gated = ssm_out * jax.nn.silu(gate_part)
    head_squares = jnp.sum(gated * gated, axis=-1)
    all_squares = lax.all_gather(head_squares, "seq", axis=1, tiled=True)
    group_means = jnp.sum(all_squares.reshape(requests, per_group, GROUPS), axis=1) / (
        per_group * head_width
    )
    own_means = jnp.einsum("hg,rg->rh", select, group_means, precision=highest)
    normed_mix = (
        gated
        * lax.rsqrt(own_means + epsilon)[..., None]
        * norm_gain.reshape(heads_here, head_width)
    ).astype(jnp.bfloat16)
    mixer_term = jnp.dot(
        normed_mix.reshape(requests, heads_here * head_width),
        out_mixer,
        preferred_element_type=jnp.float32,
    )
    mixer = lax.psum_scatter(mixer_term, "seq", scatter_dimension=1, tiled=True)
    columns = width // count_seq
    stream_cols = lax.dynamic_slice_in_dim(stream, position * columns, columns, 1)
    middle = (stream_cols + mixer).astype(jnp.bfloat16)
    middle_f = middle.astype(jnp.float32)
    scaled = (middle_f * attn_gain).astype(jnp.bfloat16)
    partial_proj = jnp.dot(scaled, w_qkv, preferred_element_type=jnp.float32)
    partial_sq = jnp.sum(middle_f * middle_f, axis=-1)
    projected, total_sq = lax.psum((partial_proj, partial_sq), "seq")
    qkv = (projected * lax.rsqrt(total_sq / width + epsilon)[:, None]).astype(jnp.bfloat16)
    group_size = QH // KVH
    queries = qkv[:, : QH * HD]
    fresh_keys = qkv[:, QH * HD : (QH + KVH) * HD].reshape(requests, KVH, HD)
    fresh_values = qkv[:, (QH + KVH) * HD :].reshape(requests, KVH, HD)
    new_kv = qkv[:, QH * HD :]
    scale = 1.0 / HD**0.5
    pages_here = kv_cache.shape[0]
    page_len = kv_cache.shape[1]
    pages_req = page_table.shape[1]
    slots = position * pages_here + jnp.arange(pages_here, dtype=jnp.int32)
    matches = page_table[None, :, :] == slots[:, None, None]
    owner_hit = jnp.any(matches, axis=2)
    owner = owner_hit.astype(jnp.bfloat16)
    logical = jnp.sum(
        jnp.any(matches, axis=1) * jnp.arange(pages_req, dtype=jnp.int32)[None, :], axis=1
    )
    page_length = jnp.sum(jnp.where(owner_hit, lengths[None, :], 0), axis=1)
    token_pos = logical[:, None] * page_len + jnp.arange(page_len, dtype=jnp.int32)[None, :]
    live = token_pos < page_length[:, None]
    page_queries = jnp.dot(owner, queries, preferred_element_type=jnp.float32).astype(jnp.bfloat16)
    page_queries = page_queries.reshape(pages_here, KVH, group_size, HD)
    cached = kv_cache.reshape(pages_here, page_len, 2, KVH, HD)
    scores = (
        jnp.einsum(
            "pgjd,ptgd->pgjt", page_queries, cached[:, :, 0], preferred_element_type=jnp.float32
        )
        * scale
    )
    live_mask = live[:, None, None, :]
    masked = jnp.where(live_mask, scores, lowest)
    page_peak = jnp.max(masked, axis=-1)
    weights = jnp.where(live_mask, jnp.exp(masked - page_peak[..., None]), 0.0)
    page_total = jnp.sum(weights, axis=-1)
    page_values = jnp.einsum(
        "pgjt,ptgd->pgjd",
        weights.astype(jnp.bfloat16),
        cached[:, :, 1],
        preferred_element_type=jnp.float32,
    )
    owner_mask = owner_hit[:, :, None, None]
    request_peak = jnp.max(jnp.where(owner_mask, page_peak[:, None], lowest), axis=0)
    factor = jnp.where(owner_mask, jnp.exp(page_peak[:, None] - request_peak[None]), 0.0)
    request_total = jnp.einsum("prgj,pgj->rgj", factor, page_total, precision=highest)
    request_values = jnp.einsum("prgj,pgjd->rgjd", factor, page_values, precision=highest)
    request_peak = request_peak.reshape(requests, QH)
    request_total = request_total.reshape(requests, QH)
    request_values = request_values.reshape(requests, QH, HD)
    query_rows = queries.reshape(requests, QH, HD)
    key_rows = jnp.repeat(fresh_keys, group_size, axis=1)
    value_rows = jnp.repeat(fresh_values, group_size, axis=1)
    peak_all, total_all, values_all = merged(
        (request_peak, request_total, request_values), "seq", merge_pair
    )
    attended = finish(
        peak_all, total_all, values_all, query_rows, key_rows, value_rows, scale
    ).reshape(requests, QH * HD)
    final = (middle_f + jnp.dot(attended, w_out, preferred_element_type=jnp.float32)).astype(
        jnp.bfloat16
    )
    return (final, new_state, new_kv)


def solution(mesh):
    placed = (
        P("grp", None),
        P(),
        P(None, "seq"),
        P(None, "seq"),
        P(None, "seq"),
        P("grp", None, "seq"),
        P("grp", None, "seq"),
        P(None, "seq"),
        P(None, "seq"),
        P("seq"),
        P("seq"),
        P("seq"),
        P("seq"),
        P("seq", None),
        P("grp", "seq", None, None),
        P("seq"),
        P("seq", None),
        P(None, "seq"),
        P(("grp", "seq"), None, None),
        P("grp", None),
        P("grp"),
    )
    return jax.shard_map(
        shards,
        mesh=mesh,
        in_specs=placed,
        out_specs=(P("grp", "seq"), P("grp", "seq", None, None), P("grp", None)),
        check_vma=False,
    )
```

profile of v0, /device:TPU:0, one launch (start us, length us, event | category | flops | bytes accessed | tf_op | source)
XLA Modules:
  0.0 282.0 jit_solution(5698425340825484725)
XLA Ops:
  12.0 1.6 convolution_bitcast_fusion.1
  13.6 23.2 %all_gather.18 = bf16[8,2048]{1,0:T(8,128)(2,1)S(1)} all-gather(bf16[8,128]{1,0:T(8,128)(2,1)S(1)} %multiply_convert_fusion.3), channel_id=1, replica_groups=mesh['grp'=2,'seq'=16] {'seq'}, dimensions={1}, use_global_device_ids=true | all-gather | bytes 34816 | tf_op jit(solution)/shard_map/all_gather | solution.py:103
  36.8 1.6 fusion.68
  41.4 1.1 multiply_exponential_fusion
  42.5 1.1 multiply_add_fusion
  44.3 17.4 %all-gather = f32[16,1,8]{2,1,0:T(1,128)S(1)} all-gather(f32[1,1,8]{2,1,0:T(1,128)S(1)} %bitcast.157), channel_id=1, replica_groups=mesh['grp'=2,'seq'=16] {'seq'}, dimensions={0}, use_global_device_ids=true | all-gather | bytes 544 | tf_op jit(solution)/shard_map/all_gather | solution.py:124
  62.0 1.9 fusion.46
  65.1 2.3 copy.80
  67.5 50.7 %reduce-scatter.2.cloned.1.call-done = f32[8,256]{1,0:T(8,128)} async-done(((f32[8,4096]{1,0:T(8,128)}), f32[8,256]{1,0:T(8,128)}) %reduce-scatter.2.cloned.1.call-update) | async-done | bytes 8208 | tf_op jit(solution)/shard_map/reduce_scatter | solution.py:139
  119.0 1.2 fusion.42
  120.3 29.5 %psum.15 = f32[8]{0:T(128)S(1)} all-reduce(f32[8]{0:T(128)S(1)} %get-tuple-element.214), channel_id=1, replica_groups=mesh['grp'=2,'seq'=16] {'seq'}, use_global_device_ids=true, to_apply=%region_12.13 | all-reduce | flops 8 | bytes 64 | tf_op jit(solution)/shard_map/psum | solution.py:147
  149.8 61.6 %all-reduce.2.cloned.1.call-done = f32[8,6144]{1,0:T(8,128)} async-done(((f32[8,6144]{1,0:T(8,128)}), f32[8,6144]{1,0:T(8,128)}) %all-reduce.2.cloned.1.call-update) | async-done | bytes 196624 | tf_op jit(solution)/shard_map/psum | solution.py:147
  211.4 1.0 multiply_convert_fusion
  212.6 1.4 fusion.73
  214.1 1.5 fusion.8
  218.7 19.5 %all_gather.21 = bf16[16,8,32]{2,1,0:T(8,128)(2,1)S(1)} all-gather(bf16[1,8,32]{2,1,0:T(8,128)(2,1)S(1)} %copy.84), channel_id=1, replica_groups=mesh['grp'=2,'seq'=16] {'seq'}, dimensions={0}, use_global_device_ids=true | all-gather | bytes 8704 | tf_op jit(solution)/shard_map/all_gather | solution.py:17
  238.2 17.8 %all_gather.20 = bf16[16,8,32]{2,1,0:T(8,128)(2,1)S(1)} all-gather(bf16[1,8,32]{2,1,0:T(8,128)(2,1)S(1)} %copy.83), channel_id=1, replica_groups=mesh['grp'=2,'seq'=16] {'seq'}, dimensions={0}, use_global_device_ids=true | all-gather | bytes 8704 | tf_op jit(solution)/shard_map/all_gather | solution.py:17
  256.9 15.8 %while.19 = (s32[]{:T(128)}, f32[8,32]{1,0:T(8,128)S(1)}, f32[8,32]{1,0:T(8,128)S(1)}, f32[8,32,128]{2,1,0:T(8,128)S(1)}, bf16[16,8,32]{2,1,0:T(8,128)(2,1)S(1)}...) while((s32[]{:T(128)}, f32[8,32]{1,0:T(8,128)S(1)}, ...), condition=%wide.region_17.18_spmd, body=%wide.region_16.17_spmd.sunk | while | flops 133125 | bytes 337047 | solution.py:25
  256.9 1.0 fusion.87
  258.0 1.0 fusion.87
  259.0 1.0 fusion.87
  260.1 1.0 fusion.87
  261.1 1.0 fusion.87
  262.2 1.0 fusion.87
  263.2 1.0 fusion.87
  264.3 1.0 fusion.87
  265.3 1.0 fusion.87
  266.4 1.0 fusion.87
  267.4 1.0 fusion.87
  268.5 1.0 fusion.87
  269.6 1.0 fusion.87
  272.9 2.6 fusion.4
  (95 shorter events, 15.8 us)
Async XLA Ops:
  7.2 111.9 %copy-start = (bf16[256,6144]{1,0:T(8,128)(2,1)S(1)}, bf16[256,6144]{1,0:T(8,128)(2,1)}, u32[]{:S(2)}) copy-start(bf16[256,6144]{1,0:T(8,128)(2,1)} %param.39) | copy-start | bytes 9437188
  7.2 56.9 %copy-start.1 = (bf16[8,4096]{1,0:T(8,128)(2,1)S(1)}, bf16[8,4096]{1,0:T(8,128)(2,1)}, u32[]{:S(2)}) copy-start(bf16[8,4096]{1,0:T(8,128)(2,1)} %param.23) | copy-start | bytes 196612
  7.2 54.9 %copy-start.5 = (f32[64]{0:T(128)S(1)}, f32[64]{0:T(128)}, u32[]{:S(2)}) copy-start(f32[64]{0:T(128)} %param.35) | copy-start | bytes 772
  7.2 57.5 %copy-start.3 = (s32[8,4]{0,1:T(4,128)S(1)}, s32[8,4]{0,1:T(4,128)}, u32[]{:S(2)}) copy-start(s32[8,4]{0,1:T(4,128)} %param.42) | copy-start | bytes 388
  7.2 111.0 %reduce-scatter.2.cloned.1.call-start = ((), (), s32[]{:S(2)}) async-start(), calls=%async_computation.1 | async-start | bytes 139264 | tf_op jit(solution)/shard_map/reduce_scatter | solution.py:139
  12.0 55.4 %copy-start.6 = (s32[8]{0:T(128)S(1)}, s32[8]{0:T(128)}, u32[]{:S(2)}) copy-start(s32[8]{0:T(128)} %param.43) | copy-start | bytes 100
  12.0 107.1 %copy-start.4 = (f32[256]{0:T(256)S(1)}, f32[256]{0:T(256)}, u32[]{:S(2)}) copy-start(f32[256]{0:T(256)} %param.38) | copy-start | bytes 3076
  43.6 76.6 %copy-start.2 = (f32[8,1,64,128]{3,2,1,0:T(8,128)}, f32[8,1,64,128]{3,2,1,0:T(8,128)S(1)}, u32[]{:S(2)}) copy-start(f32[8,1,64,128]{3,2,1,0:T(8,128)S(1)} %multiply_add_fusion) | copy-start | bytes 786436
  64.0 147.4 %all-reduce.2.cloned.1.call-start = ((), (), s32[]{:S(2)}) async-start(), calls=%async_computation.2 | async-start | bytes 393216 | tf_op jit(solution)/shard_map/psum | solution.py:147
  120.3 135.7 %all-gather.3.cloned.1.call-start = ((), (), s32[]{:S(2)}) async-start(), calls=%async_computation.3 | async-start | bytes 1114112 | tf_op jit(solution)/shard_map/all_gather | solution.py:17
Sparse Core Ops, SparseCore 0:
  64.1 54.0 reduce-scatter.1
  121.6 89.7 all-reduce.1
  217.1 36.9 all-gather.2
where the time goes:
time: 284 us; the launch traced here: 282 us
  waiting for transfers between devices  112 us (39%)
  blocking collectives  107 us (38%)
  other arithmetic  23.6 us (8%)
  between operations  15.9 us (6%)
  matrix products  14.8 us (5%)
  local copies, waits for them, and re-layouts  7.37 us (3%)
    psum x1, waiting for transfers between devices, shards(): projected, total_sq = lax.psum((partial_proj, partial_sq), 'seq')  61.6 us
    reduce_scatter x1, waiting for transfers between devices, shards(): mixer = lax.psum_scatter(mixer_term, 'seq', scatter_dimension=1, tiled=True)  50.7 us
    all_gather x2, blocking collectives, merged(): lax.all_gather(part.astype(kind), axis)  37.3 us
    psum x1, blocking collectives, shards(): projected, total_sq = lax.psum((partial_proj, partial_sq), 'seq')  29.5 us
    all_gather x1, blocking collectives, shards(): lax.all_gather(group_conv, 'seq', axis=1, tiled=True).astype(jnp.float32)  23.2 us
    all_gather x1, blocking collectives, shards(): all_squares = lax.all_gather(head_squares, 'seq', axis=1, tiled=True)  17.4 us
    add x15, other arithmetic, merge_pair(): first[2] * first_factor[..., None] + second[2] * second_factor[..., None]  15 us
  transfers between devices with their start and end apart: 3, of which 2 were waited for; matrix products, arithmetic and copies ran while one was open for 2% of the time, Pallas kernels for 0%

commit v1 on v0

--- a/solution.py
+++ b/solution.py
@@ -121,7 +121,12 @@
     )
     gated = ssm_out * jax.nn.silu(gate_part)
     head_squares = jnp.sum(gated * gated, axis=-1)
-    all_squares = lax.all_gather(head_squares, "seq", axis=1, tiled=True)
+    ring = [head_squares]
+    for hop in range(15):
+        ring.append(lax.ppermute(ring[-1], "seq", [(dev, (dev + 1) % 16) for dev in range(16)]))
+    all_squares = jnp.roll(
+        jnp.concatenate(ring[::-1], axis=1), (lax.axis_index("seq") + 1) * ring[0].shape[1], axis=1
+    )
     group_means = jnp.sum(all_squares.reshape(requests, per_group, GROUPS), axis=1) / (
         per_group * head_width
     )

time: 284 us -> 351 us (1.24)
  waiting for transfers between devices: 112 us -> 195 us
  blocking collectives: 107 us -> 90 us
    ppermute x0 -> x15, waiting for transfers between devices: none -> 80.4 us  [shards(): lax.ppermute(ring[-1], 'seq', [(dev, (dev + 1) % 16) for dev in range(16)])]
    all_gather x1 -> x0, blocking collectives: 17.4 us -> none  [shards(): all_squares = lax.all_gather(head_squares, 'seq', axis=1, tiled=True)]
  transfers between devices with their start and end apart: 3 -> 18, of which waited for: 2 -> 17; matrix products, arithmetic and copies ran while one was open for 2% -> 2% of each run, Pallas kernels for 0% -> 0%
where the time goes in v1:
time: 351 us; the launch traced here: 349 us
  waiting for transfers between devices  195 us (56%)
  blocking collectives  90 us (26%)
  other arithmetic  23.6 us (7%)
  between operations  16 us (5%)
  matrix products  14.8 us (4%)
  local copies, waits for them, and re-layouts  8.78 us (3%)
    ppermute x15, waiting for transfers between devices, shards(): lax.ppermute(ring[-1], 'seq', [(dev, (dev + 1) % 16) for dev in range(16)])  80.4 us
    psum x1, waiting for transfers between devices, shards(): projected, total_sq = lax.psum((partial_proj, partial_sq), 'seq')  61.6 us
    reduce_scatter x1, waiting for transfers between devices, shards(): mixer = lax.psum_scatter(mixer_term, 'seq', scatter_dimension=1, tiled=True)  52.9 us
    all_gather x2, blocking collectives, merged(): lax.all_gather(part.astype(kind), axis)  37.3 us
    psum x1, blocking collectives, shards(): projected, total_sq = lax.psum((partial_proj, partial_sq), 'seq')  29.5 us
    all_gather x1, blocking collectives, shards(): lax.all_gather(group_conv, 'seq', axis=1, tiled=True).astype(jnp.float32)  23.2 us
    add x15, other arithmetic, merge_pair(): first[2] * first_factor[..., None] + second[2] * second_factor[..., None]  15 us
  transfers between devices with their start and end apart: 18, of which 17 were waited for; matrix products, arithmetic and copies ran while one was open for 2% of the time, Pallas kernels for 0%

profile of v1, /device:TPU:0, one launch (start us, length us, event | category | flops | bytes accessed | tf_op | source)
XLA Modules:
  0.0 349.0 jit_solution(11654629354982226430)
XLA Ops:
  12.0 1.6 convolution_bitcast_fusion.1
  13.6 23.2 %all_gather.15 = bf16[8,2048]{1,0:T(8,128)(2,1)S(1)} all-gather(bf16[8,128]{1,0:T(8,128)(2,1)S(1)} %multiply_convert_fusion.3), channel_id=1, replica_groups=mesh['grp'=2,'seq'=16] {'seq'}, dimensions={1}, use_global_device_ids=true | all-gather | bytes 34816 | tf_op jit(solution)/shard_map/all_gather | solution.py:103
  36.8 1.6 fusion.68
  41.4 1.1 multiply_exponential_fusion
  42.5 1.1 multiply_add_fusion
  45.8 2.3 copy.173
  48.2 1.9 collective-permute-done
  50.1 5.6 %collective-permute-done.1 = f32[8,1]{0,1:T(1,128)S(1)} collective-permute-done((f32[8,1]{0,1:T(1,128)S(1)}, f32[8,1]{0,1:T(1,128)S(1)}, u32[]{:S(2)}, u32[]{:S(2)}) %collective-permute-start.1) | collective-permute-done | bytes 64 | tf_op jit(solution)/shard_map/ppermute | solution.py:126
  55.8 5.6 %collective-permute-done.2 = f32[8,1]{0,1:T(1,128)S(1)} collective-permute-done((f32[8,1]{0,1:T(1,128)S(1)}, f32[8,1]{0,1:T(1,128)S(1)}, u32[]{:S(2)}, u32[]{:S(2)}) %collective-permute-start.2) | collective-permute-done | bytes 64 | tf_op jit(solution)/shard_map/ppermute | solution.py:126
  61.5 5.6 %collective-permute-done.3 = f32[8,1]{0,1:T(1,128)S(1)} collective-permute-done((f32[8,1]{0,1:T(1,128)S(1)}, f32[8,1]{0,1:T(1,128)S(1)}, u32[]{:S(2)}, u32[]{:S(2)}) %collective-permute-start.3) | collective-permute-done | bytes 64 | tf_op jit(solution)/shard_map/ppermute | solution.py:126
  67.2 5.6 %collective-permute-done.4 = f32[8,1]{0,1:T(1,128)S(1)} collective-permute-done((f32[8,1]{0,1:T(1,128)S(1)}, f32[8,1]{0,1:T(1,128)S(1)}, u32[]{:S(2)}, u32[]{:S(2)}) %collective-permute-start.4) | collective-permute-done | bytes 64 | tf_op jit(solution)/shard_map/ppermute | solution.py:126
  72.9 5.6 %collective-permute-done.5 = f32[8,1]{0,1:T(1,128)S(1)} collective-permute-done((f32[8,1]{0,1:T(1,128)S(1)}, f32[8,1]{0,1:T(1,128)S(1)}, u32[]{:S(2)}, u32[]{:S(2)}) %collective-permute-start.5) | collective-permute-done | bytes 64 | tf_op jit(solution)/shard_map/ppermute | solution.py:126
  78.6 5.6 %collective-permute-done.6 = f32[8,1]{0,1:T(1,128)S(1)} collective-permute-done((f32[8,1]{0,1:T(1,128)S(1)}, f32[8,1]{0,1:T(1,128)S(1)}, u32[]{:S(2)}, u32[]{:S(2)}) %collective-permute-start.6) | collective-permute-done | bytes 64 | tf_op jit(solution)/shard_map/ppermute | solution.py:126
  84.3 5.6 %collective-permute-done.7 = f32[8,1]{0,1:T(1,128)S(1)} collective-permute-done((f32[8,1]{0,1:T(1,128)S(1)}, f32[8,1]{0,1:T(1,128)S(1)}, u32[]{:S(2)}, u32[]{:S(2)}) %collective-permute-start.7) | collective-permute-done | bytes 64 | tf_op jit(solution)/shard_map/ppermute | solution.py:126
  90.0 5.6 %collective-permute-done.8 = f32[8,1]{0,1:T(1,128)S(1)} collective-permute-done((f32[8,1]{0,1:T(1,128)S(1)}, f32[8,1]{0,1:T(1,128)S(1)}, u32[]{:S(2)}, u32[]{:S(2)}) %collective-permute-start.8) | collective-permute-done | bytes 64 | tf_op jit(solution)/shard_map/ppermute | solution.py:126
  95.6 5.6 %collective-permute-done.9 = f32[8,1]{0,1:T(1,128)S(1)} collective-permute-done((f32[8,1]{0,1:T(1,128)S(1)}, f32[8,1]{0,1:T(1,128)S(1)}, u32[]{:S(2)}, u32[]{:S(2)}) %collective-permute-start.9) | collective-permute-done | bytes 64 | tf_op jit(solution)/shard_map/ppermute | solution.py:126
  101.3 5.6 %collective-permute-done.10 = f32[8,1]{0,1:T(1,128)S(1)} collective-permute-done((f32[8,1]{0,1:T(1,128)S(1)}, f32[8,1]{0,1:T(1,128)S(1)}, u32[]{:S(2)}, u32[]{:S(2)}) %collective-permute-start.10) | collective-permute-done | bytes 64 | tf_op jit(solution)/shard_map/ppermute | solution.py:126
  107.0 5.6 %collective-permute-done.11 = f32[8,1]{0,1:T(1,128)S(1)} collective-permute-done((f32[8,1]{0,1:T(1,128)S(1)}, f32[8,1]{0,1:T(1,128)S(1)}, u32[]{:S(2)}, u32[]{:S(2)}) %collective-permute-start.11) | collective-permute-done | bytes 64 | tf_op jit(solution)/shard_map/ppermute | solution.py:126
  112.7 5.6 %collective-permute-done.12 = f32[8,1]{0,1:T(1,128)S(1)} collective-permute-done((f32[8,1]{0,1:T(1,128)S(1)}, f32[8,1]{0,1:T(1,128)S(1)}, u32[]{:S(2)}, u32[]{:S(2)}) %collective-permute-start.12) | collective-permute-done | bytes 64 | tf_op jit(solution)/shard_map/ppermute | solution.py:126
  118.4 5.6 %collective-permute-done.13 = f32[8,1]{0,1:T(1,128)S(1)} collective-permute-done((f32[8,1]{0,1:T(1,128)S(1)}, f32[8,1]{0,1:T(1,128)S(1)}, u32[]{:S(2)}, u32[]{:S(2)}) %collective-permute-start.13) | collective-permute-done | bytes 64 | tf_op jit(solution)/shard_map/ppermute | solution.py:126
  124.1 5.6 %collective-permute-done.14 = f32[8,1]{0,1:T(1,128)S(1)} collective-permute-done((f32[8,1]{0,1:T(1,128)S(1)}, f32[8,1]{0,1:T(1,128)S(1)}, u32[]{:S(2)}, u32[]{:S(2)}) %collective-permute-start.14) | collective-permute-done | bytes 64 | tf_op jit(solution)/shard_map/ppermute | solution.py:126
  130.2 2.0 fusion.46
  132.3 52.9 %reduce-scatter.2.cloned.1.call-done = f32[8,256]{1,0:T(8,128)} async-done(((f32[8,4096]{1,0:T(8,128)}), f32[8,256]{1,0:T(8,128)}) %reduce-scatter.2.cloned.1.call-update) | async-done | bytes 8208 | tf_op jit(solution)/shard_map/reduce_scatter | solution.py:144
  186.1 1.2 fusion.42
  187.3 29.5 %psum.15 = f32[8]{0:T(128)S(1)} all-reduce(f32[8]{0:T(128)S(1)} %get-tuple-element.214), channel_id=1, replica_groups=mesh['grp'=2,'seq'=16] {'seq'}, use_global_device_ids=true, to_apply=%region_12.13 | all-reduce | flops 8 | bytes 64 | tf_op jit(solution)/shard_map/psum | solution.py:152
  216.9 61.6 %all-reduce.2.cloned.1.call-done = f32[8,6144]{1,0:T(8,128)} async-done(((f32[8,6144]{1,0:T(8,128)}), f32[8,6144]{1,0:T(8,128)}) %all-reduce.2.cloned.1.call-update) | async-done | bytes 196624 | tf_op jit(solution)/shard_map/psum | solution.py:152
  279.6 1.4 fusion.73
  281.1 1.5 fusion.8
  285.8 19.5 %all_gather.17 = bf16[16,8,32]{2,1,0:T(8,128)(2,1)S(1)} all-gather(bf16[1,8,32]{2,1,0:T(8,128)(2,1)S(1)} %copy.177), channel_id=1, replica_groups=mesh['grp'=2,'seq'=16] {'seq'}, dimensions={0}, use_global_device_ids=true | all-gather | bytes 8704 | tf_op jit(solution)/shard_map/all_gather | solution.py:17
  305.3 17.8 %all_gather.16 = bf16[16,8,32]{2,1,0:T(8,128)(2,1)S(1)} all-gather(bf16[1,8,32]{2,1,0:T(8,128)(2,1)S(1)} %copy.176), channel_id=1, replica_groups=mesh['grp'=2,'seq'=16] {'seq'}, dimensions={0}, use_global_device_ids=true | all-gather | bytes 8704 | tf_op jit(solution)/shard_map/all_gather | solution.py:17
  323.9 15.8 %while.19 = (s32[]{:T(128)}, f32[8,32]{1,0:T(8,128)S(1)}, f32[8,32]{1,0:T(8,128)S(1)}, f32[8,32,128]{2,1,0:T(8,128)S(1)}, bf16[16,8,32]{2,1,0:T(8,128)(2,1)S(1)}...) while((s32[]{:T(128)}, f32[8,32]{1,0:T(8,128)S(1)}, ...), condition=%wide.region_17.18_spmd, body=%wide.region_16.17_spmd.sunk | while | flops 133125 | bytes 337047 | solution.py:25
  339.9 2.6 fusion.4
  (141 shorter events, 31.6 us)
Async XLA Ops:
  7.2 178.9 %copy-start = (bf16[256,6144]{1,0:T(8,128)(2,1)S(1)}, bf16[256,6144]{1,0:T(8,128)(2,1)}, u32[]{:S(2)}) copy-start(bf16[256,6144]{1,0:T(8,128)(2,1)} %param.39) | copy-start | bytes 9437188
  7.2 37.6 %copy-start.1 = (bf16[8,4096]{1,0:T(8,128)(2,1)S(1)}, bf16[8,4096]{1,0:T(8,128)(2,1)}, u32[]{:S(2)}) copy-start(bf16[8,4096]{1,0:T(8,128)(2,1)} %param.23) | copy-start | bytes 196612
  7.2 38.2 %copy-start.3 = (s32[8,4]{0,1:T(4,128)S(1)}, s32[8,4]{0,1:T(4,128)}, u32[]{:S(2)}) copy-start(s32[8,4]{0,1:T(4,128)} %param.42) | copy-start | bytes 388
  7.2 40.9 %copy-start.6 = (s32[8]{0:T(128)S(1)}, s32[8]{0:T(128)}, u32[]{:S(2)}) copy-start(s32[8]{0:T(128)} %param.43) | copy-start | bytes 100
  7.2 123.0 %copy-start.5 = (f32[64]{0:T(128)S(1)}, f32[64]{0:T(128)}, u32[]{:S(2)}) copy-start(f32[64]{0:T(128)} %param.35) | copy-start | bytes 772
  7.2 178.0 %reduce-scatter.2.cloned.1.call-start = ((), (), s32[]{:S(2)}) async-start(), calls=%async_computation.1 | async-start | bytes 139264 | tf_op jit(solution)/shard_map/reduce_scatter | solution.py:144
  13.5 172.5 %copy-start.4 = (f32[256]{0:T(256)S(1)}, f32[256]{0:T(256)}, u32[]{:S(2)}) copy-start(f32[256]{0:T(256)} %param.38) | copy-start | bytes 3076
  43.6 143.7 %copy-start.2 = (f32[8,1,64,128]{3,2,1,0:T(8,128)}, f32[8,1,64,128]{3,2,1,0:T(8,128)S(1)}, u32[]{:S(2)}) copy-start(f32[8,1,64,128]{3,2,1,0:T(8,128)S(1)} %multiply_add_fusion) | copy-start | bytes 786436
  44.3 5.7 %collective-permute-start = (f32[8,1]{0,1:T(1,128)S(1)}, f32[8,1]{0,1:T(1,128)S(1)}, u32[]{:S(2)}, u32[]{:S(2)}) collective-permute-start(f32[8,1]{0,1:T(1,128)S(1)} %bitcast.153), channel_id=1, source_target_pairs={{0,1},{1,2},{2,3},{3,4},{4,5},{5,6},{6,7},{7,8},{8,9},{9,10},{10,1... | collective-permute-start | bytes 104 | tf_op jit(solution)/shard_map/ppermute | solution.py:126
  50.0 5.7 %collective-permute-start.1 = (f32[8,1]{0,1:T(1,128)S(1)}, f32[8,1]{0,1:T(1,128)S(1)}, u32[]{:S(2)}, u32[]{:S(2)}) collective-permute-start(f32[8,1]{0,1:T(1,128)S(1)} %collective-permute-done), channel_id=1, source_target_pairs={{0,1},{1,2},{2,3},{3,4},{4,5},{5,6},{6,7},{7,8},{8,9},{9,10},{10,1... | collective-permute-start | bytes 104 | tf_op jit(solution)/shard_map/ppermute | solution.py:126
  55.7 5.7 %collective-permute-start.2 = (f32[8,1]{0,1:T(1,128)S(1)}, f32[8,1]{0,1:T(1,128)S(1)}, u32[]{:S(2)}, u32[]{:S(2)}) collective-permute-start(f32[8,1]{0,1:T(1,128)S(1)} %collective-permute-done.1), channel_id=1, source_target_pairs={{0,1},{1,2},{2,3},{3,4},{4,5},{5,6},{6,7},{7,8},{8,9},{9,10},{10,1... | collective-permute-start | bytes 104 | tf_op jit(solution)/shard_map/ppermute | solution.py:126
  61.4 5.7 %collective-permute-start.3 = (f32[8,1]{0,1:T(1,128)S(1)}, f32[8,1]{0,1:T(1,128)S(1)}, u32[]{:S(2)}, u32[]{:S(2)}) collective-permute-start(f32[8,1]{0,1:T(1,128)S(1)} %collective-permute-done.2), channel_id=1, source_target_pairs={{0,1},{1,2},{2,3},{3,4},{4,5},{5,6},{6,7},{7,8},{8,9},{9,10},{10,1... | collective-permute-start | bytes 104 | tf_op jit(solution)/shard_map/ppermute | solution.py:126
  67.1 5.7 %collective-permute-start.4 = (f32[8,1]{0,1:T(1,128)S(1)}, f32[8,1]{0,1:T(1,128)S(1)}, u32[]{:S(2)}, u32[]{:S(2)}) collective-permute-start(f32[8,1]{0,1:T(1,128)S(1)} %collective-permute-done.3), channel_id=1, source_target_pairs={{0,1},{1,2},{2,3},{3,4},{4,5},{5,6},{6,7},{7,8},{8,9},{9,10},{10,1... | collective-permute-start | bytes 104 | tf_op jit(solution)/shard_map/ppermute | solution.py:126
  72.8 5.7 %collective-permute-start.5 = (f32[8,1]{0,1:T(1,128)S(1)}, f32[8,1]{0,1:T(1,128)S(1)}, u32[]{:S(2)}, u32[]{:S(2)}) collective-permute-start(f32[8,1]{0,1:T(1,128)S(1)} %collective-permute-done.4), channel_id=1, source_target_pairs={{0,1},{1,2},{2,3},{3,4},{4,5},{5,6},{6,7},{7,8},{8,9},{9,10},{10,1... | collective-permute-start | bytes 104 | tf_op jit(solution)/shard_map/ppermute | solution.py:126
  78.5 5.7 %collective-permute-start.6 = (f32[8,1]{0,1:T(1,128)S(1)}, f32[8,1]{0,1:T(1,128)S(1)}, u32[]{:S(2)}, u32[]{:S(2)}) collective-permute-start(f32[8,1]{0,1:T(1,128)S(1)} %collective-permute-done.5), channel_id=1, source_target_pairs={{0,1},{1,2},{2,3},{3,4},{4,5},{5,6},{6,7},{7,8},{8,9},{9,10},{10,1... | collective-permute-start | bytes 104 | tf_op jit(solution)/shard_map/ppermute | solution.py:126
  84.2 5.7 %collective-permute-start.7 = (f32[8,1]{0,1:T(1,128)S(1)}, f32[8,1]{0,1:T(1,128)S(1)}, u32[]{:S(2)}, u32[]{:S(2)}) collective-permute-start(f32[8,1]{0,1:T(1,128)S(1)} %collective-permute-done.6), channel_id=1, source_target_pairs={{0,1},{1,2},{2,3},{3,4},{4,5},{5,6},{6,7},{7,8},{8,9},{9,10},{10,1... | collective-permute-start | bytes 104 | tf_op jit(solution)/shard_map/ppermute | solution.py:126
  89.9 5.7 %collective-permute-start.8 = (f32[8,1]{0,1:T(1,128)S(1)}, f32[8,1]{0,1:T(1,128)S(1)}, u32[]{:S(2)}, u32[]{:S(2)}) collective-permute-start(f32[8,1]{0,1:T(1,128)S(1)} %collective-permute-done.7), channel_id=1, source_target_pairs={{0,1},{1,2},{2,3},{3,4},{4,5},{5,6},{6,7},{7,8},{8,9},{9,10},{10,1... | collective-permute-start | bytes 104 | tf_op jit(solution)/shard_map/ppermute | solution.py:126
  95.6 5.7 %collective-permute-start.9 = (f32[8,1]{0,1:T(1,128)S(1)}, f32[8,1]{0,1:T(1,128)S(1)}, u32[]{:S(2)}, u32[]{:S(2)}) collective-permute-start(f32[8,1]{0,1:T(1,128)S(1)} %collective-permute-done.8), channel_id=1, source_target_pairs={{0,1},{1,2},{2,3},{3,4},{4,5},{5,6},{6,7},{7,8},{8,9},{9,10},{10,1... | collective-permute-start | bytes 104 | tf_op jit(solution)/shard_map/ppermute | solution.py:126
  101.3 5.7 %collective-permute-start.10 = (f32[8,1]{0,1:T(1,128)S(1)}, f32[8,1]{0,1:T(1,128)S(1)}, u32[]{:S(2)}, u32[]{:S(2)}) collective-permute-start(f32[8,1]{0,1:T(1,128)S(1)} %collective-permute-done.9), channel_id=1, source_target_pairs={{0,1},{1,2},{2,3},{3,4},{4,5},{5,6},{6,7},{7,8},{8,9},{9,10},{10,1... | collective-permute-start | bytes 104 | tf_op jit(solution)/shard_map/ppermute | solution.py:126
  106.9 5.7 %collective-permute-start.11 = (f32[8,1]{0,1:T(1,128)S(1)}, f32[8,1]{0,1:T(1,128)S(1)}, u32[]{:S(2)}, u32[]{:S(2)}) collective-permute-start(f32[8,1]{0,1:T(1,128)S(1)} %collective-permute-done.10), channel_id=1, source_target_pairs={{0,1},{1,2},{2,3},{3,4},{4,5},{5,6},{6,7},{7,8},{8,9},{9,10},{10,1... | collective-permute-start | bytes 104 | tf_op jit(solution)/shard_map/ppermute | solution.py:126
  112.6 5.7 %collective-permute-start.12 = (f32[8,1]{0,1:T(1,128)S(1)}, f32[8,1]{0,1:T(1,128)S(1)}, u32[]{:S(2)}, u32[]{:S(2)}) collective-permute-start(f32[8,1]{0,1:T(1,128)S(1)} %collective-permute-done.11), channel_id=1, source_target_pairs={{0,1},{1,2},{2,3},{3,4},{4,5},{5,6},{6,7},{7,8},{8,9},{9,10},{10,1... | collective-permute-start | bytes 104 | tf_op jit(solution)/shard_map/ppermute | solution.py:126
  118.3 5.7 %collective-permute-start.13 = (f32[8,1]{0,1:T(1,128)S(1)}, f32[8,1]{0,1:T(1,128)S(1)}, u32[]{:S(2)}, u32[]{:S(2)}) collective-permute-start(f32[8,1]{0,1:T(1,128)S(1)} %collective-permute-done.12), channel_id=1, source_target_pairs={{0,1},{1,2},{2,3},{3,4},{4,5},{5,6},{6,7},{7,8},{8,9},{9,10},{10,1... | collective-permute-start | bytes 104 | tf_op jit(solution)/shard_map/ppermute | solution.py:126
  124.0 5.7 %collective-permute-start.14 = (f32[8,1]{0,1:T(1,128)S(1)}, f32[8,1]{0,1:T(1,128)S(1)}, u32[]{:S(2)}, u32[]{:S(2)}) collective-permute-start(f32[8,1]{0,1:T(1,128)S(1)} %collective-permute-done.13), channel_id=1, source_target_pairs={{0,1},{1,2},{2,3},{3,4},{4,5},{5,6},{6,7},{7,8},{8,9},{9,10},{10,1... | collective-permute-start | bytes 104 | tf_op jit(solution)/shard_map/ppermute | solution.py:126
  132.2 146.3 %all-reduce.2.cloned.1.call-start = ((), (), s32[]{:S(2)}) async-start(), calls=%async_computation.2 | async-start | bytes 393216 | tf_op jit(solution)/shard_map/psum | solution.py:152
  187.3 135.7 %all-gather.2.cloned.1.call-start = ((), (), s32[]{:S(2)}) async-start(), calls=%async_computation.3 | async-start | bytes 1114112 | tf_op jit(solution)/shard_map/all_gather | solution.py:17
Sparse Core Ops, SparseCore 0:
  132.3 52.8 reduce-scatter.1
  188.7 89.7 all-reduce.1
  284.1 36.9 all-gather.1
